TPU v7x, 32 devices: a whole 2x2x4 slice. The times are simulated.
32 devices in a mesh: dp: 8 (over z, y), comp: 4 (over x, core).
Axes of the slice: x: 2, y: 2, z: 4, core: 2. Of those that a mesh axis runs over, the one named last changes fastest.
Arguments:
- points: float32 [8192, 64], P('dp'), may hold values from -36 to 36
- means: float32 [256, 64], P('comp'), may hold values from -6 to 6
- whiten: float32 [256, 64, 64], P('comp'), may hold values from -0.25 to 2, as said below
- log_weight: float32 [256], P('comp'), may hold values from -4 to 4
Outputs:
- new_means: float32 [256, 64], P('comp')
- new_whiten: float32 [256, 64, 64], P('comp')
- new_log_weight: float32 [256], P('comp')
- point_loglik: float32 [8192], P('dp')
Inputs may be any that keep to these rules, and one draw needn't show every extreme that they name: Each whiten[k] is lower triangular with diagonal entries between 0.5 and 2.
All inputs are finite; a program needn't handle non-finite values.
Results may differ from a plain program's by a relative error of at most 0.0003.
Values sent between devices are 32-bit elements; how exact they have to be, the bound alone decides.
A program may use at most 64 MiB of HBM per device.

v0:
```python
import math

import jax
import jax.numpy as jnp
from jax import lax
from jax.sharding import PartitionSpec as P

K = 256


HIGH = lax.Precision.HIGHEST


def refit_params(square, sums, counts, width, total_points):
    grown = counts + 1.0
    centre = sums / grown[:, None]
    eye = jnp.eye(width, dtype=jnp.float32)
    cov = (square - sums[:, :, None] * sums[:, None, :] / grown[:, None, None] + eye[None]) / grown[
        :, None, None
    ]
    chol = jnp.linalg.cholesky(cov)
    factor = lax.linalg.triangular_solve(
        chol, jnp.broadcast_to(eye, chol.shape), left_side=True, lower=True
    )
    weight = jnp.log(grown / (total_points + K))
    return (centre, factor, weight)


def body(points, means, whiten, log_weight):
    count_rows, width = points.shape
    local = means.shape[0]
    block = min(512, count_rows)
    blocks = count_rows // block
    stacked = whiten.reshape(local * width, width)
    offset = jnp.einsum("ked,kd->ke", whiten, means, precision=HIGH).reshape(local * width, 1)
    logdet = jnp.sum(jnp.log(jnp.diagonal(whiten, axis1=1, axis2=2)), axis=1)
    const = log_weight + logdet - 0.5 * width * math.log(2.0 * math.pi)
    tiles = points.reshape(blocks, block, width)

    def score(tile):
        projected = (
            lax.dot_general(stacked, tile, (((1,), (1,)), ((), ())), precision=HIGH) - offset
        )
        distance = jnp.sum((projected * projected).reshape(local, width, block), axis=1)
        return const[:, None] - 0.5 * distance

    logp = lax.map(score, tiles)
    peak = jnp.max(logp, axis=1)
    peak = lax.pmax(peak, "comp")
    partial_total = jnp.sum(jnp.exp(logp - peak[:, None, :]), axis=1)
    total = lax.psum(partial_total, "comp")
    lse = peak + jnp.log(total)
    resp = jnp.exp(logp - lse[:, None, :])

    def accumulate(carry, pieces):
        tile, weight = pieces
        outer = (tile[:, :, None] * tile[:, None, :]).reshape(block, width * width)
        scatter = carry[0] + jnp.dot(weight, outer, precision=HIGH)
        sums = carry[1] + jnp.dot(weight, tile, precision=HIGH)
        counts = carry[2] + jnp.sum(weight, axis=1)
        return ((scatter, sums, counts), None)

    columns = width * width
    start = (
        jnp.zeros((local, columns), jnp.float32),
        jnp.zeros((local, width), jnp.float32),
        jnp.zeros((local,), jnp.float32),
    )
    (scatter, sums, counts), unused = lax.scan(accumulate, start, (tiles, resp))
    total_points = count_rows * lax.axis_size("dp")
    scatter, sums, counts = (
        lax.psum_scatter(scatter, "dp", scatter_dimension=0, tiled=True),
        lax.psum_scatter(sums, "dp", scatter_dimension=0, tiled=True),
        lax.psum_scatter(counts, "dp", scatter_dimension=0, tiled=True),
    )
    centre, factor, weight = refit_params(
        scatter.reshape(scatter.shape[0], width, width), sums, counts, width, total_points
    )
    centre, factor, weight = (
        lax.all_gather(centre, "dp", axis=0, tiled=True),
        lax.all_gather(factor, "dp", axis=0, tiled=True),
        lax.all_gather(weight, "dp", axis=0, tiled=True),
    )
    return (centre, factor, weight, (lse / width).reshape(count_rows))


def solution(mesh):
    in_specs = (P("dp", None), P("comp", None), P("comp", None, None), P("comp"))
    out_specs = (P("comp", None), P("comp", None, None), P("comp"), P("dp"))
    return jax.shard_map(body, mesh=mesh, in_specs=in_specs, out_specs=out_specs, check_vma=False)
```

profile of v0, /device:TPU:0, one launch (start us, length us, event | category | flops | bytes accessed | tf_op | source)
XLA Modules:
  0.0 330.3 jit_solution(15399564940060556085)
XLA Ops:
  7.2 0.0 reduce-scatter.2.cloned.1.call-start
  7.3 1.2 reshape.97
  8.4 2.4 copy.41
  10.8 0.9 gather_fusion
  11.7 4.9 %fusion.15 = f32[64,1,64]{2,1,0:T(1,128)S(1)} fusion(f32[64,64,64]{2,1,0:T(8,128)} %param.10, f32[64,64,1]{1,2,0:T(1,128)S(1)} %bitcast.74), kind=kOutput, calls=%fused_computation.45 | convolution fusion | flops 3145728 | bytes 1081344 | tf_op jit(solution)/shard_map/ked,kd->ke/dot_general | solution.py:35
  16.7 0.1 reshape.99
  16.8 0.7 add_add_fusion
  17.4 50.3 %while.25 = (s32[]{:T(128)}, f32[2,64,512]{2,1,0:T(8,128)}, f32[64]{0:T(128)S(1)}, f32[2,512,64]{1,0,2:T(2,128)S(1)}, f32[4096,64]{1,0:T(8,128)}, /*index=5*/f32[4096,1]{0,1:T(1,128)S(1)}, s32[]{:T(128)}) while((s32[]{:T(128)}, f32[2,64,512]{2,1,0:T(8,128)}, f32[64]{0:T(128)S(1)}, f32[2,512,64]{1,0,2:T(2,128)S(1)}, f32[4096,64]{1,0:T(8,128)}, ...), condition=%wide.region_3.4_spmd, body=%wide.region_1.3_spmd.sunk | while | flops 1616936960 | bytes 37765772 | solution.py:47
  17.4 0.1 constant_dynamic-slice_fusion.6
  17.6 0.1 copy.63
  17.7 10.3 %multiply_bitcast_fusion.3 = f32[4096,512]{0,1:T(8,128)} fusion(f32[4096,64]{1,0:T(8,128)} %get-tuple-element.263, f32[4096]{0:T(1024)S(1)} %bitcast.78, f32[1,512,64]{2,1,0:T(8,128)S(1)} %copy.63), kind=kOutput, calls=%fused_computation.2.clone.1 | convolution fusion | flops 1614807040 | bytes 9584640 | tf_op jit(solution)/shard_map/while/body/eval_jaxpr/dot_general | solution.py:42
  28.0 9.0 %copy.64 = f32[4096,512]{1,0:T(8,128)} copy(f32[4096,512]{0,1:T(8,128)} %multiply_bitcast_fusion.3) | data formatting | bytes 16777216 | tf_op jit(solution)/shard_map/while/body/eval_jaxpr/mul | solution.py:44
  37.0 4.8 %bitcast_reduce_fusion.2 = f32[64,512]{1,0:T(8,128)S(1)} fusion(f32[4096,512]{1,0:T(8,128)} %copy.64), kind=kLoop, calls=%fused_computation.1.clone.1 | loop fusion | flops 2064384 | bytes 8519680 | tf_op jit(solution)/shard_map/while/body/eval_jaxpr/reduce_sum | solution.py:44
  41.8 0.1 fusion.29
  41.9 0.7 copy-done.3
  42.6 0.1 constant_dynamic-slice_fusion.6
  42.7 0.1 copy.63
  42.8 10.3 %multiply_bitcast_fusion.3 = f32[4096,512]{0,1:T(8,128)} fusion(f32[4096,64]{1,0:T(8,128)} %get-tuple-element.263, f32[4096]{0:T(1024)S(1)} %bitcast.78, f32[1,512,64]{2,1,0:T(8,128)S(1)} %copy.63), kind=kOutput, calls=%fused_computation.2.clone.1 | convolution fusion | flops 1614807040 | bytes 9584640 | tf_op jit(solution)/shard_map/while/body/eval_jaxpr/dot_general | solution.py:42
  53.2 9.0 %copy.64 = f32[4096,512]{1,0:T(8,128)} copy(f32[4096,512]{0,1:T(8,128)} %multiply_bitcast_fusion.3) | data formatting | bytes 16777216 | tf_op jit(solution)/shard_map/while/body/eval_jaxpr/mul | solution.py:44
  62.1 4.8 %bitcast_reduce_fusion.2 = f32[64,512]{1,0:T(8,128)S(1)} fusion(f32[4096,512]{1,0:T(8,128)} %copy.64), kind=kLoop, calls=%fused_computation.1.clone.1 | loop fusion | flops 2064384 | bytes 8519680 | tf_op jit(solution)/shard_map/while/body/eval_jaxpr/reduce_sum | solution.py:44
  66.9 0.1 fusion.29
  67.0 0.7 copy-done.3
  67.7 1.0 reduce_max.9
  68.7 8.4 %pmax.7 = f32[2,512]{1,0:T(2,128)S(1)} all-reduce(f32[2,512]{1,0:T(2,128)S(1)} %reduce_max.9), channel_id=1, replica_groups=mesh['dp'=8,'comp'=4] {'comp'}, use_global_device_ids=true, to_apply=%region_5.6 | all-reduce | flops 1024 | bytes 8192 | tf_op jit(solution)/shard_map/pmax | solution.py:49
  77.1 1.0 exponential_reduce_fusion
  78.1 5.8 %psum.7 = f32[2,512]{1,0:T(2,128)S(1)} all-reduce(f32[2,512]{1,0:T(2,128)S(1)} %exponential_reduce_fusion), channel_id=1, replica_groups=mesh['dp'=8,'comp'=4] {'comp'}, use_global_device_ids=true, to_apply=%region_7.8 | all-reduce | flops 1024 | bytes 8192 | tf_op jit(solution)/shard_map/psum | solution.py:51
  83.9 1.0 subtract_exponential_fusion
  84.9 30.5 %while.26 = (s32[]{:T(128)}, f32[64,4096]{1,0:T(8,128)S(1)}, f32[64,64]{1,0:T(8,128)S(1)}, f32[64]{0:T(128)S(1)}, f32[2,64,512]{2,1,0:T(8,128)S(1)}, /*index=5*/f32[2,512,64]{1,0,2:T(2,128)S(1)}, s32[]{:T(128)}, s32[]{:T(128)}) while((s32[]{:T(128)}, f32[64,4096]{1,0:T(8,128)S(1)}, f32[64,64]{1,0:T(8,128)S(1)}, ...), condition=%wide.region_10.11_spmd.clone, body=%wide.region_8.10_spmd.clone.sunk | while | flops 1638441088 | bytes 20104304 | solution.py:69
  84.9 0.1 constant_dynamic-slice_fusion.7
  85.0 4.3 %broadcast_multiply_fusion.2 = f32[512,64,64]{0,2,1:T(8,128)} fusion(f32[512,64]{0,1:T(8,128)S(1)} %bitcast.77), kind=kLoop, calls=%fused_computation.8.clone.1 | loop fusion | flops 2097152 | bytes 8519680 | tf_op jit(solution)/shard_map/while/body/eval_jaxpr/mul | solution.py:57
  89.4 10.3 %convolution_add_fusion.4 = f32[64,4096]{1,0:T(8,128)S(1)} fusion(f32[512,4096]{0,1:T(8,128)} %bitcast.75, f32[64,4096]{1,0:T(8,128)S(1)} %get-tuple-element.275, pred[]{:T(512)S(6)} %compare.11, f32[2,64,512]{2,1,0:T(8,128)S(1)} %get-tuple-element.286, s32[]{:T(128)} %get-tuple-element.274), kind=kOutput, calls=%fused_computation.7.clone.1 | convolution fusion | flops 1611137024 | bytes 10616837 | tf_op jit(solution)/shard_map/while/body/eval_jaxpr/dot_general | solution.py:58
  99.7 0.3 convolution_add_fusion.5
  100.0 0.1 dynamic-slice_reduce_fusion.2
  100.1 0.1 constant_dynamic-slice_fusion.7
  100.3 4.3 %broadcast_multiply_fusion.2 = f32[512,64,64]{0,2,1:T(8,128)} fusion(f32[512,64]{0,1:T(8,128)S(1)} %bitcast.77), kind=kLoop, calls=%fused_computation.8.clone.1 | loop fusion | flops 2097152 | bytes 8519680 | tf_op jit(solution)/shard_map/while/body/eval_jaxpr/mul | solution.py:57
  104.6 10.3 %convolution_add_fusion.4 = f32[64,4096]{1,0:T(8,128)S(1)} fusion(f32[512,4096]{0,1:T(8,128)} %bitcast.75, f32[64,4096]{1,0:T(8,128)S(1)} %get-tuple-element.275, pred[]{:T(512)S(6)} %compare.11, f32[2,64,512]{2,1,0:T(8,128)S(1)} %get-tuple-element.286, s32[]{:T(128)} %get-tuple-element.274), kind=kOutput, calls=%fused_computation.7.clone.1 | convolution fusion | flops 1611137024 | bytes 10616837 | tf_op jit(solution)/shard_map/while/body/eval_jaxpr/dot_general | solution.py:58
  114.9 0.3 convolution_add_fusion.5
  115.2 0.1 dynamic-slice_reduce_fusion.2
  115.4 1.0 copy-done.1
  116.3 0.0 reduce-scatter.2.cloned.1.call-update
  116.4 0.0 all-gather.2.cloned.1.call-start
  116.4 0.1 copy.45
  116.5 0.6 fusion.14
  118.4 21.9 %all-reduce.2 = f32[64]{0:T(128)S(1)} all-reduce(f32[64]{0:T(128)S(1)} %get-tuple-element.72), channel_id=3, replica_groups=mesh['dp'=8,'comp'=4] {'dp'}, use_global_device_ids=true, to_apply=%region_12.13.clone | all-reduce | flops 64 | bytes 512
  140.3 0.2 log_dynamic-update-slice_fusion
  140.5 33.9 %all-reduce.3 = (f32[64,64]{1,0:T(8,128)S(1)}, f32[64]{0:T(128)}) all-reduce(f32[64,64]{1,0:T(8,128)S(1)} %get-tuple-element.71, f32[64]{0:T(128)S(1)} %get-tuple-element.167), channel_id=2, replica_groups=mesh['dp'=8,'comp'=4] {'dp'}, use_global_device_ids=true, to_apply=%region_11.12.clone | all-reduce | flops 4160 | bytes 33280
  174.4 0.1 broadcast_divide_fusion
  174.5 7.4 %reduce-scatter.2.cloned.1.call-done = f32[8,4096]{1,0:T(8,128)} async-done(((f32[64,4096]{1,0:T(8,128)}), f32[8,4096]{1,0:T(8,128)}) %reduce-scatter.2.cloned.1.call-update) | async-done | bytes 131088 | tf_op jit(solution)/shard_map/reduce_scatter | solution.py:72
  181.9 1.0 reshape.100
  182.9 0.1 copy.44
  183.0 0.1 add_divide_fusion
  183.2 0.1 copy.46
  183.3 0.1 fusion.11
  183.5 46.9 %custom-call.7 = f32[8,64,64]{2,1,0:T(8,128)S(1)} custom-call(f32[8,64,64]{2,1,0:T(8,128)S(1)} %fusion.11), custom_call_target="Cholesky" | custom-call | tf_op jit(solution)/shard_map/jit(cholesky)/cholesky | solution.py:21
  230.4 0.1 compare_reduce_fusion
  230.6 0.1 select_bitcast_fusion
  230.7 39.3 %custom-call.8 = f32[8,1,64,64]{2,3,1,0:T(8,128)S(1)} custom-call(f32[8,1,64,64]{3,2,1,0:T(8,128)S(1)} %select_bitcast_fusion), custom_call_target="InvertDiagBlocksLowerTriangular" | custom-call | tf_op jit(solution)/shard_map/triangular_solve | solution.py:22
  270.0 1.3 fusion.9
  271.3 0.0 all-gather.2.cloned.1.call-update
  271.3 30.9 %all_gather.9 = f32[64,64]{1,0:T(8,128)S(1)} all-gather(f32[8,64]{1,0:T(8,128)S(1)} %get-tuple-element.165), channel_id=1, replica_groups=mesh['dp'=8,'comp'=4] {'dp'}, dimensions={0}, use_global_device_ids=true | all-gather | bytes 18432 | tf_op jit(solution)/shard_map/all_gather | solution.py:80
  302.2 0.6 copy.55
  302.8 16.9 %all-gather.2.cloned.1.call-done = f32[64,64,64]{2,1,0:T(8,128)} async-done(((f32[8,64,64]{2,1,0:T(8,128)}), f32[64,64,64]{2,1,0:T(8,128)}) %all-gather.2.cloned.1.call-update) | async-done | bytes 1048592 | tf_op jit(solution)/shard_map/all_gather | solution.py:81
  319.7 0.6 copy.89
  320.3 3.2 copy.90
  (27 shorter events, 0.2 us)
Async XLA Ops:
  7.2 4.6 %copy-start = (f32[64,64]{1,0:T(8,128)S(1)}, f32[64,64]{1,0:T(8,128)}, u32[]{:S(2)}) copy-start(f32[64,64]{1,0:T(8,128)} %param.9) | copy-start | bytes 49156
  7.2 174.7 %reduce-scatter.2.cloned.1.call-start = ((), (), s32[]{:S(2)}) async-start(), calls=%async_computation.1 | async-start | bytes 1179648 | tf_op jit(solution)/shard_map/reduce_scatter | solution.py:72
  37.0 4.8 %copy-start.2 = (f32[2,64,512]{2,1,0:T(8,128)S(1)}, f32[2,64,512]{2,1,0:T(8,128)}, u32[]{:S(2)}) copy-start(f32[2,64,512]{2,1,0:T(8,128)} %get-tuple-element.253) | copy-start | bytes 786436 | tf_op jit(solution)/shard_map/while
  41.9 0.7 copy-start.3
  62.1 4.8 %copy-start.2 = (f32[2,64,512]{2,1,0:T(8,128)S(1)}, f32[2,64,512]{2,1,0:T(8,128)}, u32[]{:S(2)}) copy-start(f32[2,64,512]{2,1,0:T(8,128)} %get-tuple-element.253) | copy-start | bytes 786436 | tf_op jit(solution)/shard_map/while
  67.0 0.7 copy-start.3
  84.9 31.7 %copy-start.4 = (u32[32]{0:T(128)S(1)}, u32[32]{0:T(128)}, u32[]{:S(2)}) copy-start(u32[32]{0:T(128)} %constant.106) | copy-start | bytes 388
  115.4 1.0 copy-start.1
  116.4 203.3 %all-gather.2.cloned.1.call-start = ((), (), s32[]{:S(2)}) async-start(), calls=%async_computation.2 | async-start | bytes 2359296 | tf_op jit(solution)/shard_map/all_gather | solution.py:81
Sparse Core Ops, SparseCore 0:
  116.5 65.3 reduce-scatter.1
  271.5 48.1 all-gather.1
where the time goes:
time: 331 us; the launch traced here: 330 us
  other arithmetic  109 us (33%)
  blocking collectives  101 us (31%)
  matrix products  48.1 us (15%)
  local copies, waits for them, and re-layouts  31.9 us (10%)
  waiting for transfers between devices  24.3 us (7%)
  between operations  15.5 us (5%)
    unnamed x2, blocking collectives  55.8 us
    another operation x4, other arithmetic, refit_params(): chol = jnp.linalg.cholesky(cov)  47.1 us
    another operation x3, other arithmetic, refit_params(): lax.linalg.triangular_solve(chol, jnp.broadcast_to(eye, chol.shape), left...  39.4 us
    all_gather x1, blocking collectives, body(): lax.all_gather(centre, 'dp', axis=0, tiled=True)  30.9 us
    dot_general x2, matrix products, accumulate(): scatter = carry[0] + jnp.dot(weight, outer, precision=HIGH)  20.7 us
    dot_general x2, matrix products, score(): lax.dot_general(stacked, tile, (((1,), (1,)), ((), ())), precision=HIGH)  20.6 us
    mul x2, local copies, waits for them, and re-layouts, score(): projected * projected  18 us
    all_gather x1, waiting for transfers between devices, body(): lax.all_gather(factor, 'dp', axis=0, tiled=True)  16.9 us
  transfers between devices with their start and end apart: 2, of which 2 were waited for; matrix products, arithmetic and copies ran while one was open for 0% of the time, Pallas kernels for 0%

commit v1 on v0

v1 whole, which is shorter than its diff:
```python
import functools
import math

import jax
import jax.numpy as jnp
from jax import lax
from jax.experimental import pallas as pl
from jax.experimental.pallas import tpu as pltpu
from jax.sharding import PartitionSpec as P

MESH = pl.DeviceIdType.MESH
F32 = jnp.float32
BF16 = jnp.bfloat16


def split2(v):
    high = v.astype(BF16)
    mid = (v - high.astype(F32)).astype(BF16)
    return high, mid


def split3(v):
    high = v.astype(BF16)
    rest = v - high.astype(F32)
    mid = rest.astype(BF16)
    low = (rest - mid.astype(F32)).astype(BF16)
    return high, mid, low


def lanes(shape):
    return lax.broadcasted_iota(jnp.int32, shape, len(shape) - 1)


def kernel(n_dp, pair, n_comp, total_points, total_k, xt_ref, means_ref, whiten_ref, lw_ref,
           out_ref, tail_ref, lse_ref, lwc_ref, xcat_ref, logp_ref, stat_ref, resp_ref, send_ref, yrecv_ref, recv_ref,
           mat_ref, inv_ref, stat_send, stat_recv, y_send, y_recv, rs_send, rs_recv, ag_send, ag_recv, fw_send, fw_recv):
    local, width = means_ref.shape
    count = xt_ref.shape[1]
    far = n_dp // pair
    own = local // n_dp
    half = width // 2
    quarter = width // 4
    eighth = width // 8
    n_rows = send_ref.shape[2]
    me = lax.axis_index("dp")
    mc = lax.axis_index("comp")
    a, b = me // pair, lax.rem(me, pair)
    other = pair - 1 - b
    partner = a * pair + other

    barrier = pltpu.get_barrier_semaphore()

    def greet(d, carry):
        pl.semaphore_signal(barrier, inc=1, device_id={"dp": lax.rem(me + d, n_dp)}, device_id_type=MESH)
        return carry

    lax.fori_loop(1, n_dp, greet, 0)
    for d in range(1, n_comp):
        pl.semaphore_signal(barrier, inc=1, device_id={"comp": lax.rem(mc + d, n_comp)}, device_id_type=MESH)

    xh, xm, xl = split3(xt_ref[...])
    square = (local, local)
    diagonal = lax.broadcasted_iota(jnp.int32, square, 0) == lax.broadcasted_iota(jnp.int32, square, 1)
    lwc_ref[...] = jnp.sum(jnp.where(diagonal, lw_ref[...], 0.0), axis=1, keepdims=True)
    xcat_ref[...] = jnp.concatenate([xh, xm, xh, xm, xl, xh, xl, xm], axis=0)

    group = 8 if local % 8 == 0 else local

    def score(c, carry):
        rows = pl.ds(pl.multiple_of(c * group, group), group)
        w = whiten_ref[rows]
        m = means_ref[rows, :]
        offset = jnp.sum(w * m[:, None, :], axis=2, keepdims=True).reshape(group * width, 1)
        shape = (group, width, width)
        eye = lax.broadcasted_iota(jnp.int32, shape, 1) == lax.broadcasted_iota(jnp.int32, shape, 2)
        diag = jnp.sum(jnp.where(eye, w, 0.0), axis=1)
        const = lwc_ref[rows, :] + jnp.sum(jnp.log(diag), axis=1, keepdims=True) - 0.5 * width * math.log(2.0 * math.pi)
        wh, wm, wl = split3(w.reshape(group * width, width))
        wcat = jnp.concatenate([wh, wh, wm, wm, wh, wl, wm, wl], axis=1)
        projected = jnp.dot(wcat, xcat_ref[...], preferred_element_type=F32) - offset
        distance = jnp.sum((projected * projected).reshape(group, width, count), axis=1)
        logp_ref[rows, :] = const - 0.5 * distance
        return carry

    lax.fori_loop(0, local // group, score, 0)

    logp = logp_ref[...]
    top = jnp.max(logp, axis=0, keepdims=True)
    stat_ref[0, 0:1, :] = top
    stat_ref[0, 1:2, :] = jnp.sum(jnp.exp(logp - top), axis=0, keepdims=True)

    pl.semaphore_wait(barrier, n_dp - 1 + n_comp - 1)

    def stat_copy(d):
        return pltpu.make_async_remote_copy(
            src_ref=stat_ref.at[0], dst_ref=stat_ref.at[d], send_sem=stat_send.at[d], recv_sem=stat_recv.at[d],
            device_id={"comp": lax.rem(mc + d, n_comp)}, device_id_type=MESH)

    for d in range(1, n_comp):
        stat_copy(d).start()
    for d in range(1, n_comp):
        stat_copy(d).wait()

    peak = stat_ref[0, 0:1, :]
    for d in range(1, n_comp):
        peak = jnp.maximum(peak, stat_ref[d, 0:1, :])
    total = jnp.zeros_like(peak)
    for d in range(n_comp):
        total = total + stat_ref[d, 1:2, :] * jnp.exp(stat_ref[d, 0:1, :] - peak)
    lse = peak + jnp.log(total)
    lse_ref[...] = lse / width
    resp = jnp.exp(logp_ref[...] - lse)
    resp_ref[...] = jnp.concatenate(split3(resp), axis=0)

    contract = (((1,), (1,)), ((), ()))

    def weighted(outer):
        high, mid, low = split3(outer)
        first = lax.dot_general(resp_ref[...], high, contract, preferred_element_type=F32)
        second = lax.dot_general(resp_ref[0:2 * local, :], mid, contract, preferred_element_type=F32)
        third = lax.dot_general(resp_ref[0:local, :], low, contract, preferred_element_type=F32)
        small = (first[2 * local:3 * local] + second[local:2 * local]) + third
        return small + (first[local:2 * local] + second[0:local]) + first[0:local]

    def keep(row, value):
        value = value.reshape(far, pair, own, value.shape[1])
        for side in range(pair):
            send_ref[side, :, pl.ds(row, 1)] = value[:, side][:, None]

    def upper(g, carry):
        t = 2 * g
        parts = [xt_ref[pl.ds(i, 1), :] * xt_ref[...] for i in (t, t + quarter, t + 1, t + 1 + quarter)]
        value = weighted(jnp.concatenate(parts, axis=0))
        keep(t, value[:, 0:2 * width])
        keep(t + 1, value[:, 2 * width:4 * width])
        return carry

    def lower(g, carry):
        t = 2 * g
        right = xt_ref[half:width, :]
        parts = [xt_ref[pl.ds(half + q * eighth + s, 1), :] * right for s in (t, t + 1) for q in range(4)]
        value = weighted(jnp.concatenate(parts, axis=0))
        keep(quarter + t, value[:, 0:2 * width])
        keep(quarter + t + 1, value[:, 2 * width:4 * width])
        return carry

    def y_copy(part, lo, size):
        return pltpu.make_async_remote_copy(
            src_ref=send_ref.at[other, :, pl.ds(lo, size)], dst_ref=yrecv_ref.at[:, pl.ds(lo, size)],
            send_sem=y_send.at[part], recv_sem=y_recv.at[part], device_id={"dp": partner}, device_id_type=MESH)

    def z_copy(part, lo, size, d):
        peer = lax.rem(a + d, far)
        return pltpu.make_async_remote_copy(
            src_ref=send_ref.at[b, peer, pl.ds(lo, size)], dst_ref=recv_ref.at[d, pl.ds(lo, size)],
            send_sem=rs_send.at[part, d], recv_sem=rs_recv.at[part, d],
            device_id={"dp": peer * pair + b}, device_id_type=MESH)

    def z_start(part, lo, size):
        if pair > 1:
            y_copy(part, lo, size).wait()
            send_ref[b, :, lo:lo + size] = send_ref[b, :, lo:lo + size] + yrecv_ref[:, lo:lo + size]

        def step(d, carry):
            z_copy(part, lo, size, d).start()
            return carry
        lax.fori_loop(1, far, step, 0)

    piece = eighth
    step_rows = quarter // 4
    parts = [(2 * piece, piece + 1)] + [(c * step_rows, step_rows) for c in range(4)]
    keep(n_rows - 1, weighted(jnp.concatenate([xt_ref[...], jnp.ones_like(xt_ref[...])], axis=0)))
    for part, (lo, size) in enumerate(parts):
        if part == 0:
            lax.fori_loop(0, piece // 2, lower, 0)
        else:
            lax.fori_loop(lo // 2, (lo + size) // 2, upper, 0)
        if pair > 1:
            y_copy(part, lo, size).start()
        if part > 0:
            z_start(part - 1, *parts[part - 1])
    z_start(len(parts) - 1, *parts[-1])
    for part, (lo, size) in enumerate(parts):
        def step(d, carry, part=part, lo=lo, size=size):
            z_copy(part, lo, size, d).wait()
            return carry
        lax.fori_loop(1, far, step, 0)

    def add(d, acc):
        return acc + recv_ref[d]

    recv_ref[0] = lax.fori_loop(1, far, add, send_ref[b, a])

    lane = lanes((own, 2 * width))
    tail = recv_ref[0, n_rows - 1]
    back = pltpu.roll(tail, width, 1)
    grown_low = back + 1.0
    grown = jnp.where(lane < width, back, tail) + 1.0
    sums = jnp.where(lane < width, tail, 0.0)
    centre = sums / grown
    for i in range(width):
        if i < quarter:
            row = recv_ref[0, i]
        elif i < half:
            row = pltpu.roll(recv_ref[0, i - quarter], width, 1)
        else:
            q, s = divmod(i - half, eighth)
            row = recv_ref[0, quarter + s]
            shift = (half - q * half) % (2 * width)
            if shift:
                row = pltpu.roll(row, shift, 1)
        row = jnp.where(lane < width, row, 0.0) - sums[:, i:i + 1] * centre
        mat_ref[i] = row + jnp.where((lane == i) | (lane == width + i), 1.0, 0.0)

    def spread(row, i):
        return jnp.broadcast_to(row[:, i:i + 1], row.shape)

    for j in range(0, width, 2):
        p, q = mat_ref[j], mat_ref[j + 1]
        cross = spread(p, j + 1)
        inv_p = 1.0 / spread(p, j)
        ratio = cross * inv_p
        clean = q - ratio * p
        inv_q = 1.0 / (spread(q, j + 1) - ratio * cross)
        p_scaled, q_scaled = p * inv_p, clean * inv_q
        inv_ref[j] = pltpu.roll(p, width, 1) * jnp.sqrt(grown * inv_p)
        inv_ref[j + 1] = pltpu.roll(clean, width, 1) * jnp.sqrt(grown * inv_q)
        for i in range(j + 2, width):
            u = spread(p, i)
            v = spread(q, i) - ratio * u
            mat_ref[i] = mat_ref[i] - u * p_scaled - v * q_scaled

    for t in range(quarter):
        first, second = inv_ref[half + t], inv_ref[half + quarter + t]
        packed = jnp.where(lane < width, first, pltpu.roll(second, width, 1))
        out_ref[me, :, pl.ds(t, 1), :] = packed[:, None, :]
    for t in range(eighth):
        packed = inv_ref[t]
        for q in range(1, 4):
            packed = jnp.where((lane >= q * half) & (lane < (q + 1) * half),
                               pltpu.roll(inv_ref[q * eighth + t], q * half, 1), packed)
        out_ref[me, :, pl.ds(quarter + t, 1), :] = packed[:, None, :]
    tail_ref[me] = jnp.where(lane < width, centre, jnp.log(grown / (total_points + total_k)))

    def ag_copies(d):
        to = lax.rem(a + d, far) * pair + b
        return [pltpu.make_async_remote_copy(
            src_ref=ref.at[me], dst_ref=ref.at[me], send_sem=ag_send.at[k, d], recv_sem=ag_recv.at[k, d],
            device_id={"dp": to}, device_id_type=MESH) for k, ref in enumerate((out_ref, tail_ref))]

    def fw_copies(d):
        block = lax.rem(a - d + far, far) * pair + b
        return [pltpu.make_async_remote_copy(
            src_ref=ref.at[block], dst_ref=ref.at[block], send_sem=fw_send.at[k, d], recv_sem=fw_recv.at[k, d],
            device_id={"dp": partner}, device_id_type=MESH) for k, ref in enumerate((out_ref, tail_ref))]

    def ag_start(d, carry):
        for copy in ag_copies(d):
            copy.start()
        return carry

    def forward(d, carry):
        for copy in ag_copies(d):
            copy.wait()
        if pair > 1:
            for copy in fw_copies(d):
                copy.start()
        return carry

    def fw_wait(d, carry):
        for copy in fw_copies(d):
            copy.wait()
        return carry

    lax.fori_loop(1, far, ag_start, 0)
    if pair > 1:
        for copy in fw_copies(0):
            copy.start()
    lax.fori_loop(1, far, forward, 0)
    if pair > 1:
        lax.fori_loop(0, far, fw_wait, 0)


def finish(packed_ref, tail_ref, lse_in_ref, means_ref, factor_ref, lw_ref, lse_ref):
    local, width = means_ref.shape
    half, quarter, eighth = width // 2, width // 4, width // 8
    lse_ref[...] = lse_in_ref[...]
    tail = tail_ref[...]
    means_ref[...] = tail[:, :width]
    square = (local, local)
    diagonal = lax.broadcasted_iota(jnp.int32, square, 0) == lax.broadcasted_iota(jnp.int32, square, 1)
    lw_ref[...] = jnp.sum(jnp.where(diagonal, tail[:, width:width + 1], 0.0), axis=0, keepdims=True)

    def step(k, carry):
        bottom = packed_ref[k, 0:quarter, :]
        factor_ref[k, half:half + quarter, :] = bottom[:, :width]
        factor_ref[k, half + quarter:width, :] = pltpu.roll(bottom, width, 1)[:, :width]
        top = packed_ref[k, quarter:quarter + eighth, :]
        lane = lanes(top.shape)
        for q in range(4):
            row = pltpu.roll(top, (4 - q) * half, 1) if q else top
            factor_ref[k, q * eighth:(q + 1) * eighth, :] = jnp.where(lane < half, row, 0.0)[:, :width]
        return carry

    lax.fori_loop(0, local, step, 0, unroll=8)


def body(n_dp, n_comp, points, means, whiten, log_weight):
    count, width = points.shape
    local = means.shape[0]
    own = local // n_dp
    half, quarter, eighth = width // 2, width // 4, width // 8
    n_rows = quarter + eighth + 1
    pair = 2 if n_dp % 2 == 0 else 1
    far = n_dp // pair
    vmem = pl.BlockSpec(memory_space=pltpu.VMEM)
    shape = jax.ShapeDtypeStruct
    packed, tail, lse = pl.pallas_call(
        functools.partial(kernel, n_dp, pair, n_comp, count * n_dp, local * n_comp),
        out_shape=(shape((n_dp, own, n_rows - 1, 2 * width), F32), shape((n_dp, own, 2 * width), F32), shape((1, count), F32)),
        in_specs=[vmem] * 4,
        out_specs=(vmem,) * 3,
        scratch_shapes=[
            pltpu.VMEM((local, 1), F32),
            pltpu.VMEM((8 * width, count), BF16),
            pltpu.VMEM((local, count), F32),
            pltpu.VMEM((n_comp, 2, count), F32),
            pltpu.VMEM((3 * local, count), BF16),
            pltpu.VMEM((pair, far, n_rows, own, 2 * width), F32),
            pltpu.VMEM((far, n_rows, own, 2 * width), F32),
            pltpu.VMEM((far, n_rows, own, 2 * width), F32),
            pltpu.VMEM((width, own, 2 * width), F32),
            pltpu.VMEM((width, own, 2 * width), F32),
            pltpu.SemaphoreType.DMA((n_comp,)),
            pltpu.SemaphoreType.DMA((n_comp,)),
            pltpu.SemaphoreType.DMA((5,)),
            pltpu.SemaphoreType.DMA((5,)),
            pltpu.SemaphoreType.DMA((5, far)),
            pltpu.SemaphoreType.DMA((5, far)),
            pltpu.SemaphoreType.DMA((2, far)),
            pltpu.SemaphoreType.DMA((2, far)),
            pltpu.SemaphoreType.DMA((2, far)),
            pltpu.SemaphoreType.DMA((2, far)),
        ],
        compiler_params=pltpu.CompilerParams(collective_id=0, has_side_effects=True),
        name="em_step",
    )(points.T, means, whiten, log_weight.reshape(1, local))
    centre, factor, weight, lse = pl.pallas_call(
        finish,
        out_shape=(shape((local, width), F32), shape((local, width, width), F32), shape((1, local), F32), shape((1, count), F32)),
        in_specs=[vmem] * 3,
        out_specs=(vmem,) * 4,
        name="finish",
    )(packed.reshape(local, n_rows - 1, 2 * width), tail.reshape(local, 2 * width), lse)
    return centre, factor, weight.reshape(local), lse.reshape(count)


def solution(mesh):
    n_dp, n_comp = mesh.shape["dp"], mesh.shape["comp"]
    in_specs = (P("dp", None), P("comp", None), P("comp", None, None), P("comp"))
    out_specs = (P("comp", None), P("comp", None, None), P("comp"), P("dp"))
    return jax.shard_map(functools.partial(body, n_dp, n_comp), mesh=mesh, in_specs=in_specs, out_specs=out_specs, check_vma=False)
```

time: 331 us -> 58.9 us (0.18)
  other arithmetic: 109 us -> 0 us
  blocking collectives: 101 us -> 0 us
  Pallas kernels: 0 us -> 58.1 us
  matrix products: 48.1 us -> 0 us
  local copies, waits for them, and re-layouts: 31.9 us -> 0 us
  waiting for transfers between devices: 24.3 us -> 0 us
  between operations: 15.5 us -> 0.64 us
    another operation x7 -> x0, other arithmetic: 86.5 us -> none  [the longest x4 47.1 us: refit_params(): chol = jnp.linalg.cholesky(cov)]
    pallas_call x0 -> x2, Pallas kernels: none -> 58.1 us  [the longest x1 54.6 us: body(): pl.pallas_call(functools.partial(kernel, n_dp, pair, n_comp, count * n_dp...]
    unnamed x2 -> x0, blocking collectives: 55.8 us -> none
    dot_general x7 -> x0, matrix products: 46.8 us -> none  [the longest x2 20.7 us: accumulate(): scatter = carry[0] + jnp.dot(weight, outer, precision=HIGH)]
    all_gather x1 -> x0, blocking collectives: 30.9 us -> none  [body(): lax.all_gather(centre, 'dp', axis=0, tiled=True)]
    mul x2 -> x0, local copies, waits for them, and re-layouts: 18 us -> none  [score(): projected * projected]
    all_gather x1 -> x0, waiting for transfers between devices: 16.9 us -> none  [body(): lax.all_gather(factor, 'dp', axis=0, tiled=True)]
    reduce_sum x6 -> x0, other arithmetic: 10.8 us -> none  [the longest x2 9.5 us: score(): jnp.sum((projected * projected).reshape(local, width, block), axis=1)]
  transfers between devices with their start and end apart: 2 -> 0, of which waited for: 2 -> 0; matrix products, arithmetic and copies ran while one was open for 0% -> 0% of each run, Pallas kernels for 0% -> 0%
where the time goes in v1:
time: 58.9 us; the launch traced here: 58.7 us
  Pallas kernels  58.1 us (99%)
  between operations  0.64 us (1%)
    pallas_call x1, Pallas kernels, body(): pl.pallas_call(functools.partial(kernel, n_dp, pair, n_comp, count * n_dp...  54.6 us
    pallas_call x1, Pallas kernels, body(): pl.pallas_call(finish, out_shape=(shape((local, width), F32), shape((loca...  3.46 us

profile of v1, /device:TPU:0, one launch (start us, length us, event | category | flops | bytes accessed | tf_op | source)
XLA Modules:
  0.0 58.7 jit_solution(17286113333248361288)
XLA Ops:
  0.6 54.6 %em_step.1 = (f32[8,8,24,128]{3,2,1,0:T(8,128)}, f32[8,8,128]{2,1,0:T(8,128)}, f32[1,1024]{1,0:T(1,128)}) custom-call(f32[64,1024]{1,0:T(8,128)} %bitcast.7, f32[64,64]{1,0:T(8,128)} %means_ref.1, f32[64,64,64]{2,1,0:T(8,128)} %whiten_ref.1, f32[1,64]{1,0:T(1,128)} %bitcast.9), custom_call_target="tpu_custom_call" | custom-call | tf_op jit(solution)/shard_map/em_step/pallas_call | solution.py:318
  55.3 3.5 %finish.1 = (f32[64,64]{1,0:T(8,128)}, f32[64,64,64]{2,1,0:T(8,128)}, f32[1,64]{1,0:T(1,128)}, f32[1,1024]{1,0:T(1,128)}) custom-call(f32[64,24,128]{2,1,0:T(8,128)} %bitcast.6, f32[64,128]{1,0:T(8,128)} %bitcast.8, f32[1,1024]{1,0:T(1,128)} %get-tuple-element.13.lse_in_ref), custom_call_target="tpu_custom_call" | custom-call | tf_op jit(solution)/shard_map/finish/pallas_call | solution.py:348

commit v2 on v1

--- a/solution.py
+++ b/solution.py
@@ -215,6 +215,62 @@
     def spread(row, i):
         return jnp.broadcast_to(row[:, i:i + 1], row.shape)
 
+    def piece_of(k, block):
+        return tail_ref.at[block] if k == 3 else out_ref.at[block, :, pl.ds(k * eighth, eighth)]
+
+    def ag_copy(k, d):
+        to = lax.rem(a + d, far) * pair + b
+        return pltpu.make_async_remote_copy(
+            src_ref=piece_of(k, me), dst_ref=piece_of(k, me), send_sem=ag_send.at[k, d], recv_sem=ag_recv.at[k, d],
+            device_id={"dp": to}, device_id_type=MESH)
+
+    def fw_copy(k, d):
+        block = lax.rem(a - d + far, far) * pair + b
+        return pltpu.make_async_remote_copy(
+            src_ref=piece_of(k, block), dst_ref=piece_of(k, block), send_sem=fw_send.at[k, d], recv_sem=fw_recv.at[k, d],
+            device_id={"dp": partner}, device_id_type=MESH)
+
+    def ag_begin(k):
+        def step(d, carry):
+            ag_copy(k, d).start()
+            return carry
+        lax.fori_loop(1, far, step, 0)
+        if pair > 1:
+            fw_copy(k, 0).start()
+
+    def ag_forward(k):
+        def step(d, carry):
+            ag_copy(k, d).wait()
+            if pair > 1:
+                fw_copy(k, d).start()
+            return carry
+        lax.fori_loop(1, far, step, 0)
+
+    def ag_end(k):
+        def step(d, carry):
+            fw_copy(k, d).wait()
+            return carry
+        if pair > 1:
+            lax.fori_loop(0, far, step, 0)
+
+    def pack_two(k, base):
+        for t in range(eighth):
+            packed = jnp.where(lane < width, inv_ref[base + t], pltpu.roll(inv_ref[base + eighth + t], width, 1))
+            out_ref[me, :, pl.ds(k * eighth + t, 1), :] = packed[:, None, :]
+        ag_begin(k)
+
+    def pack_four():
+        for t in range(eighth):
+            packed = inv_ref[t]
+            for q in range(1, 4):
+                packed = jnp.where((lane >= q * half) & (lane < (q + 1) * half),
+                                   pltpu.roll(inv_ref[q * eighth + t], q * half, 1), packed)
+            out_ref[me, :, pl.ds(t, 1), :] = packed[:, None, :]
+        ag_begin(0)
+
+    tail_ref[me] = jnp.where(lane < width, centre, jnp.log(grown / (total_points + total_k)))
+    ag_begin(3)
+
     for j in range(0, width, 2):
         p, q = mat_ref[j], mat_ref[j + 1]
         cross = spread(p, j + 1)
@@ -229,56 +285,17 @@
             u = spread(p, i)
             v = spread(q, i) - ratio * u
             mat_ref[i] = mat_ref[i] - u * p_scaled - v * q_scaled
-
-    for t in range(quarter):
-        first, second = inv_ref[half + t], inv_ref[half + quarter + t]
-        packed = jnp.where(lane < width, first, pltpu.roll(second, width, 1))
-        out_ref[me, :, pl.ds(t, 1), :] = packed[:, None, :]
-    for t in range(eighth):
-        packed = inv_ref[t]
-        for q in range(1, 4):
-            packed = jnp.where((lane >= q * half) & (lane < (q + 1) * half),
-                               pltpu.roll(inv_ref[q * eighth + t], q * half, 1), packed)
-        out_ref[me, :, pl.ds(quarter + t, 1), :] = packed[:, None, :]
-    tail_ref[me] = jnp.where(lane < width, centre, jnp.log(grown / (total_points + total_k)))
-
-    def ag_copies(d):
-        to = lax.rem(a + d, far) * pair + b
-        return [pltpu.make_async_remote_copy(
-            src_ref=ref.at[me], dst_ref=ref.at[me], send_sem=ag_send.at[k, d], recv_sem=ag_recv.at[k, d],
-            device_id={"dp": to}, device_id_type=MESH) for k, ref in enumerate((out_ref, tail_ref))]
-
-    def fw_copies(d):
-        block = lax.rem(a - d + far, far) * pair + b
-        return [pltpu.make_async_remote_copy(
-            src_ref=ref.at[block], dst_ref=ref.at[block], send_sem=fw_send.at[k, d], recv_sem=fw_recv.at[k, d],
-            device_id={"dp": partner}, device_id_type=MESH) for k, ref in enumerate((out_ref, tail_ref))]
-
-    def ag_start(d, carry):
-        for copy in ag_copies(d):
-            copy.start()
-        return carry
-
-    def forward(d, carry):
-        for copy in ag_copies(d):
-            copy.wait()
-        if pair > 1:
-            for copy in fw_copies(d):
-                copy.start()
-        return carry
-
-    def fw_wait(d, carry):
-        for copy in fw_copies(d):
-            copy.wait()
-        return carry
-
-    lax.fori_loop(1, far, ag_start, 0)
-    if pair > 1:
-        for copy in fw_copies(0):
-            copy.start()
-    lax.fori_loop(1, far, forward, 0)
-    if pair > 1:
-        lax.fori_loop(0, far, fw_wait, 0)
+        if j + 2 == half:
+            pack_four()
+        if j + 2 == half + quarter:
+            pack_two(1, half)
+            ag_forward(3)
+            ag_forward(0)
+    pack_two(2, half + quarter)
+    ag_forward(1)
+    ag_forward(2)
+    for k in range(4):
+        ag_end(k)
 
 
 def finish(packed_ref, tail_ref, lse_in_ref, means_ref, factor_ref, lw_ref, lse_ref):
@@ -292,10 +309,12 @@
     lw_ref[...] = jnp.sum(jnp.where(diagonal, tail[:, width:width + 1], 0.0), axis=0, keepdims=True)
 
     def step(k, carry):
-        bottom = packed_ref[k, 0:quarter, :]
-        factor_ref[k, half:half + quarter, :] = bottom[:, :width]
-        factor_ref[k, half + quarter:width, :] = pltpu.roll(bottom, width, 1)[:, :width]
-        top = packed_ref[k, quarter:quarter + eighth, :]
+        for piece in range(2):
+            base = half + piece * quarter
+            rows = packed_ref[k, (1 + piece) * eighth:(2 + piece) * eighth, :]
+            factor_ref[k, base:base + eighth, :] = rows[:, :width]
+            factor_ref[k, base + eighth:base + quarter, :] = pltpu.roll(rows, width, 1)[:, :width]
+        top = packed_ref[k, 0:eighth, :]
         lane = lanes(top.shape)
         for q in range(4):
             row = pltpu.roll(top, (4 - q) * half, 1) if q else top
@@ -337,10 +356,10 @@
             pltpu.SemaphoreType.DMA((5,)),
             pltpu.SemaphoreType.DMA((5, far)),
             pltpu.SemaphoreType.DMA((5, far)),
-            pltpu.SemaphoreType.DMA((2, far)),
-            pltpu.SemaphoreType.DMA((2, far)),
-            pltpu.SemaphoreType.DMA((2, far)),
-            pltpu.SemaphoreType.DMA((2, far)),
+            pltpu.SemaphoreType.DMA((4, far)),
+            pltpu.SemaphoreType.DMA((4, far)),
+            pltpu.SemaphoreType.DMA((4, far)),
+            pltpu.SemaphoreType.DMA((4, far)),
         ],
         compiler_params=pltpu.CompilerParams(collective_id=0, has_side_effects=True),
         name="em_step",

time: 58.9 us -> 60.3 us (1.024)
  Pallas kernels: 58.1 us -> 59.5 us
    pallas_call x1, Pallas kernels: 54.6 us -> 56 us  [body(): pl.pallas_call(functools.partial(kernel, n_dp, pair, n_comp, count * n_dp...]
where the time goes in v2:
time: 60.3 us; the launch traced here: 60.1 us
  Pallas kernels  59.5 us (99%)
  between operations  0.64 us (1%)
    pallas_call x1, Pallas kernels, body(): pl.pallas_call(functools.partial(kernel, n_dp, pair, n_comp, count * n_dp...  56 us
    pallas_call x1, Pallas kernels, body(): pl.pallas_call(finish, out_shape=(shape((local, width), F32), shape((loca...  3.46 us

profile of v2, /device:TPU:0, one launch (start us, length us, event | category | flops | bytes accessed | tf_op | source)
XLA Modules:
  0.0 60.1 jit_solution(16370490917841591283)
XLA Ops:
  0.6 56.0 %em_step.1 = (f32[8,8,24,128]{3,2,1,0:T(8,128)}, f32[8,8,128]{2,1,0:T(8,128)}, f32[1,1024]{1,0:T(1,128)}) custom-call(f32[64,1024]{1,0:T(8,128)} %bitcast.7, f32[64,64]{1,0:T(8,128)} %means_ref.1, f32[64,64,64]{2,1,0:T(8,128)} %whiten_ref.1, f32[1,64]{1,0:T(1,128)} %bitcast.9), custom_call_target="tpu_custom_call" | custom-call | tf_op jit(solution)/shard_map/em_step/pallas_call | solution.py:337
  56.6 3.5 %finish.1 = (f32[64,64]{1,0:T(8,128)}, f32[64,64,64]{2,1,0:T(8,128)}, f32[1,64]{1,0:T(1,128)}, f32[1,1024]{1,0:T(1,128)}) custom-call(f32[64,24,128]{2,1,0:T(8,128)} %bitcast.6, f32[64,128]{1,0:T(8,128)} %bitcast.8, f32[1,1024]{1,0:T(1,128)} %get-tuple-element.13.lse_in_ref), custom_call_target="tpu_custom_call" | custom-call | tf_op jit(solution)/shard_map/finish/pallas_call | solution.py:367
